TPU v7x, 32 devices: a whole 2x2x4 slice. The times are simulated.
32 devices in a mesh: dp: 16 (over z, y, core), rep: 2 (over x).
Axes of the slice: x: 2, y: 2, z: 4, core: 2. Of those that a mesh axis runs over, the one named last changes fastest.
Arguments:
- gate_pre: bfloat16 [2, 2048, 5632], P(None, 'dp', 'rep'), may hold values from -8 to 8
- up_pre: bfloat16 [2, 2048, 5632], P(None, 'dp', 'rep'), may hold values from -6 to 6
- out_grad: bfloat16 [2, 2048, 1024], P(None, 'dp'), may hold values from -6 to 6
- master: float32 [1024, 5632], P('dp', 'rep'), may hold values from -0.078125 to 0.078125
- moment_one: float32 [1024, 5632], P('dp', 'rep'), may hold values from -0.02 to 0.02
- moment_two: float32 [1024, 5632], P('dp', 'rep'), may hold values from 1e-06 to 1e-05
Outputs:
- layer_out: bfloat16 [2, 2048, 1024], P(None, 'dp', 'rep')
- gate_grad: bfloat16 [2, 2048, 5632], P(None, 'dp', 'rep')
- up_grad: bfloat16 [2, 2048, 5632], P(None, 'dp', 'rep')
- master_new: float32 [1024, 5632], P('dp', 'rep')
- moment_one_new: float32 [1024, 5632], P('dp', 'rep')
- moment_two_new: float32 [1024, 5632], P('dp', 'rep')
All inputs are finite; a program needn't handle non-finite values.
Results may differ from a plain program's by a relative error of at most 0.0048.
The roundings to bfloat16 on the way count: a program that leaves them out, or rounds other values in their place, can miss the bound.
Values may be sent and summed in bfloat16 or wider, within the bound.
A program may use at most 128 MiB of HBM per device.

v0:
```python
import jax
import jax.numpy as jnp
from jax import lax
from jax.sharding import PartitionSpec as P

first_power = 2.6561398887587544e-05
second_power = 0.005920529220333997


def grad_rows(cotangent, hidden):
    return lax.dot_general(
        cotangent, hidden, (((0,), (0,)), ((), ())), preferred_element_type=jnp.float32
    )


def on_device(gate_pre, up_pre, out_grad, master, moment_one, moment_two):
    shard_bf = master.astype(jnp.bfloat16)
    weights = lax.all_gather(shard_bf, "dp", axis=0, tiled=True)
    micro = gate_pre.shape[0]
    total = micro * gate_pre.shape[1] * lax.axis_size("dp")
    own_rows = master.shape[0]
    outs_list = []
    gate_list = []
    up_list = []
    hidden_list = []
    grad_sum = None
    for index in range(micro):
        gate = gate_pre[index].astype(jnp.float32)
        up_val = up_pre[index].astype(jnp.float32)
        sig = jax.nn.sigmoid(gate)
        hidden = (gate * sig * up_val).astype(jnp.bfloat16)
        hidden_list.append(hidden)
        partial_out = lax.dot_general(
            hidden, weights, (((1,), (1,)), ((), ())), preferred_element_type=jnp.float32
        )
        outs_list.append(
            lax.psum_scatter(partial_out, "rep", scatter_dimension=1, tiled=True).astype(
                jnp.bfloat16
            )
        )
        hid_grad = jnp.dot(out_grad[index], weights, preferred_element_type=jnp.float32)
        gate_list.append(
            (hid_grad * up_val * sig * (1.0 + gate * (1.0 - sig))).astype(jnp.bfloat16)
        )
        up_list.append((hid_grad * gate * sig).astype(jnp.bfloat16))

        def single_term(start, count, cotangent=out_grad[index], current=hidden):
            return grad_rows(cotangent, current)

        shard_grad = lax.psum_scatter(
            single_term(jnp.int32(0), lax.axis_size("dp") * own_rows),
            "dp",
            scatter_dimension=0,
            tiled=True,
        )
        grad_sum = shard_grad if grad_sum is None else grad_sum + shard_grad
    main_grad = grad_sum / jnp.float32(total)
    first = 0.9 * moment_one + 0.1 * main_grad
    second = 0.95 * moment_two + 0.05 * main_grad * main_grad
    update = first / (1.0 - first_power) / (jnp.sqrt(second / (1.0 - second_power)) + 1e-08)
    master_new = master - 0.003 * (update + 0.1 * master)
    return (
        jnp.stack(outs_list),
        jnp.stack(gate_list),
        jnp.stack(up_list),
        master_new,
        first,
        second,
    )


def solution(mesh):
    placed = (
        P(None, "dp", "rep"),
        P(None, "dp", "rep"),
        P(None, "dp", None),
        P("dp", "rep"),
        P("dp", "rep"),
        P("dp", "rep"),
    )
    return jax.shard_map(
        on_device,
        mesh=mesh,
        in_specs=placed,
        out_specs=(
            P(None, "dp", "rep"),
            P(None, "dp", "rep"),
            P(None, "dp", "rep"),
            P("dp", "rep"),
            P("dp", "rep"),
            P("dp", "rep"),
        ),
        check_vma=False,
    )
```

profile of v0, /device:TPU:0, one launch (start us, length us, event | category | flops | bytes accessed | tf_op | source)
XLA Modules:
  0.0 264.3 jit_solution(14178496637402104767)
XLA Ops:
  7.2 0.0 copy-start
  7.2 0.0 copy-start.1
  7.2 0.0 copy-start.3
  7.2 0.0 reduce-scatter.10.cloned.1.call-start
  7.2 3.2 %fusion.45 = f32[2816,1024]{1,0:T(8,128)S(1)} fusion(bf16[2,128,2816]{2,1,0:T(8,128)(2,1)} %param.7, bf16[2,128,2816]{2,1,0:T(8,128)(2,1)} %param.6, bf16[2,128,1024]{2,1,0:T(8,128)(2,1)} %param.8), kind=kOutput, calls=%fused_computation.56 | convolution fusion | flops 741081088 | bytes 13238272 | tf_op jit(solution)/shard_map/dot_general | solution.py:11
  10.5 0.0 copy-done
  10.5 0.0 copy-done.1
  10.5 0.0 copy-done.3
  10.5 6.0 %add_bitcast_fusion = f32[1024,2816]{0,1:T(8,128)} fusion(f32[2816,1024]{1,0:T(8,128)S(1)} %fusion.45, bf16[2,128,2816]{2,1,0:T(8,128)(2,1)S(1)} %copy-done, bf16[2,128,2816]{2,1,0:T(8,128)(2,1)S(1)} %copy-done.1, bf16[2,128,1024]{2,1,0:T(8,128)(2,1)S(1)} %copy-done.3), kind=kOutput, calls=%fused_computation | convolution fusion | flops 743964672 | bytes 24772608 | tf_op jit(solution)/shard_map/dot_general | solution.py:11
  16.5 12.0 %copy.29 = f32[1024,2816]{1,0:T(8,128)} copy(f32[1024,2816]{0,1:T(8,128)} %add_bitcast_fusion) | data formatting | bytes 23068672
  28.4 0.0 reduce-scatter.10.cloned.1.call-update
  28.5 0.0 all-gather.2.cloned.1.call-start
  28.5 129.9 %reduce-scatter.10.cloned.1.call-done = f32[64,2816]{1,0:T(8,128)} async-done(((f32[1024,2816]{1,0:T(8,128)}), f32[64,2816]{1,0:T(8,128)}) %reduce-scatter.10.cloned.1.call-update) | async-done | bytes 720912 | tf_op jit(solution)/shard_map/reduce_scatter | solution.py:50
  158.4 3.8 %multiply_subtract_fusion = (f32[64,2816]{1,0:T(8,128)}, f32[64,2816]{1,0:T(8,128)}, f32[64,2816]{1,0:T(8,128)}, bf16[64,2816]{1,0:T(8,128)(2,1)}) fusion(f32[64,2816]{1,0:T(8,128)} %param.9, f32[64,2816]{1,0:T(8,128)} %reduce-scatter.10.cloned.1.call-done, f32[64,2816]{1,0:T(8,128)} %param.10, f32[64,2816]{1,0:T(8,128)} %param.11), kind=kLoop, calls=%fused_computation.58 | loop fusion | flops 3063808 | bytes 5406720 | tf_op jit(solution)/shard_map/sub | solution.py:61
  162.2 0.0 all-gather.2.cloned.1.call-update
  162.2 0.0 reduce-scatter.8.cloned.1.call-start
  162.3 58.1 %all-gather.2.cloned.1.call-done = bf16[1024,2816]{1,0:T(8,128)(2,1)} async-done(((bf16[64,2816]{1,0:T(8,128)(2,1)}), bf16[1024,2816]{1,0:T(8,128)(2,1)}) %all-gather.2.cloned.1.call-update) | async-done | bytes 5767184 | tf_op jit(solution)/shard_map/all_gather | solution.py:18
  220.4 5.4 %fusion.40 = f32[128,1024]{1,0:T(8,128)} fusion(bf16[1024,2816]{1,0:T(8,128)(2,1)} %all-gather.2.cloned.1.call-done, bf16[2,128,2816]{2,1,0:T(8,128)(2,1)S(1)} %copy-done, bf16[2,128,2816]{2,1,0:T(8,128)(2,1)S(1)} %copy-done.1), kind=kOutput, calls=%fused_computation.53 | convolution fusion | flops 741081088 | bytes 7733248 | tf_op jit(solution)/shard_map/dot_general | solution.py:33
  225.8 0.0 reduce-scatter.8.cloned.1.call-update
  225.8 0.0 reduce-scatter.6.cloned.1.call-start
  225.9 5.4 %fusion.42 = f32[128,1024]{1,0:T(8,128)} fusion(bf16[1024,2816]{1,0:T(8,128)(2,1)} %all-gather.2.cloned.1.call-done, bf16[2,128,2816]{2,1,0:T(8,128)(2,1)S(1)} %copy-done, bf16[2,128,2816]{2,1,0:T(8,128)(2,1)S(1)} %copy-done.1), kind=kOutput, calls=%fused_computation.54 | convolution fusion | flops 741081088 | bytes 7733248 | tf_op jit(solution)/shard_map/dot_general | solution.py:33
  231.3 0.0 slice-start
  231.3 0.0 reduce-scatter.6.cloned.1.call-update
  231.3 0.0 slice-start.1
  231.3 0.0 copy-start.2
  231.4 3.7 %fusion.64 = f32[128,2816]{1,0:T(8,128)S(1)} fusion(bf16[1024,2816]{1,0:T(8,128)(2,1)} %all-gather.2.cloned.1.call-done, bf16[2,128,1024]{2,1,0:T(8,128)(2,1)S(1)} %copy-done.3), kind=kOutput, calls=%fused_computation.77 | convolution fusion | flops 738197504 | bytes 7471104 | tf_op jit(solution)/shard_map/dot_general | solution.py:41
  235.1 0.0 slice-done
  235.1 0.6 slice-done.1
  235.7 0.4 copy-done.2
  236.1 2.1 fusion.52
  238.2 1.8 pad_maximum_fusion
  240.0 0.0 reduce-scatter.8.cloned.1.call-done
  240.0 1.0 convert_bitcast_fusion.4
  241.0 15.1 %reduce-scatter.6.cloned.1.call-done = f32[128,512]{1,0:T(8,128)} async-done(((f32[128,1024]{1,0:T(8,128)}), f32[128,512]{1,0:T(8,128)}) %reduce-scatter.6.cloned.1.call-update) | async-done | bytes 262160 | tf_op jit(solution)/shard_map/reduce_scatter | solution.py:37
  256.0 1.0 convert_bitcast_fusion.5
  257.0 0.7 pad_maximum_fusion.2
  (1 shorter events, 0.0 us)
Async XLA Ops:
  7.2 3.3 %copy-start = (bf16[2,128,2816]{2,1,0:T(8,128)(2,1)S(1)}, bf16[2,128,2816]{2,1,0:T(8,128)(2,1)}, u32[]{:S(2)}) copy-start(bf16[2,128,2816]{2,1,0:T(8,128)(2,1)} %param.7) | copy-start | bytes 4325380
  7.2 3.3 %copy-start.1 = (bf16[2,128,2816]{2,1,0:T(8,128)(2,1)S(1)}, bf16[2,128,2816]{2,1,0:T(8,128)(2,1)}, u32[]{:S(2)}) copy-start(bf16[2,128,2816]{2,1,0:T(8,128)(2,1)} %param.6) | copy-start | bytes 4325380
  7.2 3.3 %copy-start.3 = (bf16[2,128,1024]{2,1,0:T(8,128)(2,1)S(1)}, bf16[2,128,1024]{2,1,0:T(8,128)(2,1)}, u32[]{:S(2)}) copy-start(bf16[2,128,1024]{2,1,0:T(8,128)(2,1)} %param.8) | copy-start | bytes 1572868
  7.2 151.2 %reduce-scatter.10.cloned.1.call-start = ((), (), s32[]{:S(2)}) async-start(), calls=%async_computation.6 | async-start | bytes 12255232 | tf_op jit(solution)/shard_map/reduce_scatter | solution.py:50
  28.5 191.9 %all-gather.2.cloned.1.call-start = ((), (), s32[]{:S(2)}) async-start(), calls=%async_computation.3 | async-start | bytes 6127616 | tf_op jit(solution)/shard_map/all_gather | solution.py:18
  162.2 77.8 %reduce-scatter.8.cloned.1.call-start = ((), (), s32[]{:S(2)}) async-start(), calls=%async_computation.5 | async-start | bytes 786432 | tf_op jit(solution)/shard_map/reduce_scatter | solution.py:37
  225.8 30.2 %reduce-scatter.6.cloned.1.call-start = ((), (), s32[]{:S(2)}) async-start(), calls=%async_computation.4 | async-start | bytes 786432 | tf_op jit(solution)/shard_map/reduce_scatter | solution.py:37
  231.3 3.8 %slice-start = ((s8[5767168]{0:T(1024)(128)(4,1)}), s8[1572864]{0:T(1024)(128)(4,1)S(1)}, s32[]{:S(2)}) async-start(s8[5767168]{0:T(1024)(128)(4,1)} %bitcast.145), calls=%async_computation.7 | async-start | bytes 3145728
  231.3 4.3 %slice-start.1 = ((s8[5767168]{0:T(1024)(128)(4,1)}), s8[4194304]{0:T(1024)(128)(4,1)S(1)}, s32[]{:S(2)}) async-start(s8[5767168]{0:T(1024)(128)(4,1)} %bitcast.145), calls=%async_computation.8 | async-start | bytes 8388608
  231.3 4.7 %copy-start.2 = (bf16[2,128,2816]{2,1,0:T(8,128)(2,1)S(1)}, bf16[2,128,2816]{2,1,0:T(8,128)(2,1)}, u32[]{:S(2)}) copy-start(bf16[2,128,2816]{2,1,0:T(8,128)(2,1)} %param.6) | copy-start | bytes 4325380
Sparse Core Ops, SparseCore 0:
  28.6 129.7 reduce-scatter.9
  162.3 57.9 all-gather.1
  225.9 13.2 reduce-scatter.7
  241.3 14.6 reduce-scatter.5
where the time goes:
time: 265 us; the launch traced here: 264 us
  waiting for transfers between devices  203 us (77%)
  matrix products  25.9 us (10%)
  between operations  13.9 us (5%)
  local copies, waits for them, and re-layouts  13 us (5%)
  other arithmetic  8.28 us (3%)
    reduce_scatter x1, waiting for transfers between devices, on_device(): lax.psum_scatter(single_term(jnp.int32(0), lax.axis_size('dp') * own_rows...  130 us
    all_gather x1, waiting for transfers between devices, on_device(): weights = lax.all_gather(shard_bf, 'dp', axis=0, tiled=True)  58.1 us
    reduce_scatter x2, waiting for transfers between devices, on_device(): lax.psum_scatter(partial_out, 'rep', scatter_dimension=1, tiled=True)  15.1 us
    unnamed x13, local copies, waits for them, and re-layouts  13 us
    dot_general x2, matrix products, on_device(): lax.dot_general(hidden, weights, (((1,), (1,)), ((), ())), preferred_elem...  10.9 us
    dot_general x2, matrix products, grad_rows(): lax.dot_general(cotangent, hidden, (((0,), (0,)), ((), ())), preferred_el...  9.21 us
    dot_general x2, matrix products, on_device(): jnp.dot(out_grad[index], weights, preferred_element_type=jnp.float32)  5.76 us
  transfers between devices with their start and end apart: 4, of which 3 were waited for; matrix products, arithmetic and copies ran while one was open for 5% of the time, Pallas kernels for 0%

commit v1 on v0

v1 whole, which is shorter than its diff:
```python
import functools

import jax
import jax.numpy as jnp
from jax import lax
from jax.experimental import pallas as pl
from jax.experimental.pallas import tpu as pltpu
from jax.sharding import PartitionSpec as P

first_power = 2.6561398887587544e-05
second_power = 0.005920529220333997

MESH = pl.DeviceIdType.MESH
CORES = 2
MID = 2


def adam(main_grad, master, moment_one, moment_two):
    first = 0.9 * moment_one + 0.1 * main_grad
    second = 0.95 * moment_two + 0.05 * main_grad * main_grad
    update = first / (1.0 - first_power) / (jnp.sqrt(second / (1.0 - second_power)) + 1e-08)
    return master - 0.003 * (update + 0.1 * master), first, second


def fused(
    outer, total,
    gate_ref, up_ref, cot_ref, cot_rows_ref, shard_ref, master_ref, one_ref, two_ref,
    out_ref, gate_grad_ref, up_grad_ref, master_new_ref, first_ref, second_ref,
    weights, hid, hid_peer, cot_peer, own_sum, mid_send, mid_recv, outer_send, outer_recv,
    part_send, part_recv,
    w_recv, w_mid_send, w_outer_send, w_core_send,
    core_send_sem, core_recv_sem,
    mid_send_sem, mid_recv_sem, outer_send_sem, outer_recv_sem, part_send_sem, part_recv_sem,
):
    me = lax.axis_index("dp")
    rep = lax.axis_index("rep")
    core = lax.rem(me, CORES)
    mid = lax.rem(me // CORES, MID)
    out = me // (CORES * MID)
    n = outer * MID * CORES
    rows, ff = shard_ref.shape
    tokens = gate_ref.shape[0]
    width = 256 if ff % 256 == 0 else 128
    chunks = ff // width

    def at(o, m, c):
        return (o * MID + m) * CORES + c

    core_peer = {"dp": at(out, mid, 1 - core)}
    mid_peer = {"dp": at(out, 1 - mid, core)}
    rep_peer = {"rep": 1 - rep}

    def outer_at(k):
        return lax.rem(out + k, outer)

    def outer_peer(k):
        return {"dp": at(outer_at(k), mid, core)}

    def remote(src, dst, send, recv, device):
        return pltpu.make_async_remote_copy(
            src_ref=src, dst_ref=dst, send_sem=send, recv_sem=recv,
            device_id=device, device_id_type=MESH,
        )

    barrier = pltpu.get_barrier_semaphore()
    peers = [core_peer, mid_peer, rep_peer] + [outer_peer(k) for k in range(1, outer)]
    for peer in peers:
        pl.semaphore_signal(barrier, inc=1, device_id=peer, device_id_type=MESH)
    pl.semaphore_wait(barrier, len(peers))

    order = sorted(range(1, outer), key=lambda k: min(k, outer - k))
    started = []

    def go(copy):
        copy.start()
        started.append(copy)
        return copy

    for k in order:
        go(remote(shard_ref, weights.at[me], w_outer_send.at[k], w_recv.at[me], outer_peer(k)))
    go(remote(shard_ref, weights.at[me], w_mid_send.at[0], w_recv.at[me], mid_peer))
    go(remote(shard_ref, weights.at[me], w_core_send.at[0], w_recv.at[me], core_peer))
    cot_copy = go(remote(cot_rows_ref.at[1 - core], cot_peer, core_send_sem.at[0], core_recv_sem.at[0], core_peer))
    weights[me] = shard_ref[...]

    def columns(j):
        return pl.ds(pl.multiple_of(j * width, width), width)

    def hidden_step(j, carry):
        cols = columns(j)
        gate = gate_ref[:, cols].astype(jnp.float32)
        sig = jax.nn.sigmoid(gate)
        hid[:, cols] = (gate * sig * up_ref[:, cols].astype(jnp.float32)).astype(jnp.bfloat16)
        return carry

    lax.fori_loop(0, chunks, hidden_step, 0)
    hid_copy = go(remote(hid, hid_peer, core_send_sem.at[1], core_recv_sem.at[1], core_peer))
    cot_copy.wait_recv()
    hid_copy.wait_recv()

    def grad_of(which, cols):
        own = cot_rows_ref[core, which].reshape(outer * rows, tokens)
        other = cot_peer[which].reshape(outer * rows, tokens)
        value = jnp.dot(own, hid[:, cols], preferred_element_type=jnp.float32)
        value += jnp.dot(other, hid_peer[:, cols], preferred_element_type=jnp.float32)
        return value.reshape(outer, rows, width)

    def send_step(j, carry):
        cols = columns(j)
        mid_send[:, :, cols] = grad_of(1 - mid, cols).astype(jnp.bfloat16)
        return carry

    lax.fori_loop(0, chunks, send_step, 0)
    shift = list(reversed(order)) + [0]
    for k in shift:
        slot = outer_at(k)
        go(remote(mid_send.at[slot], mid_recv.at[slot], mid_send_sem.at[k], mid_recv_sem.at[slot], mid_peer))

    def own_step(j, carry):
        cols = columns(j)
        own_sum[:, :, cols] = grad_of(mid, cols)
        return carry

    lax.fori_loop(0, chunks, own_step, 0)

    def arrival(slot):
        return remote(weights.at[slot], weights.at[slot], w_core_send.at[0], w_recv.at[slot], core_peer)

    def forward_outer(k):
        slot = at(lax.rem(out + outer - k, outer), mid, core)
        arrival(slot).wait_recv()
        go(remote(weights.at[slot], weights.at[slot], w_mid_send.at[k], w_recv.at[slot], mid_peer))
        go(remote(weights.at[slot], weights.at[slot], w_core_send.at[k], w_recv.at[slot], core_peer))

    def forward_mid(k):
        slot = at(lax.rem(out + outer - k, outer), 1 - mid, core)
        arrival(slot).wait_recv()
        go(remote(weights.at[slot], weights.at[slot], w_core_send.at[outer + k], w_recv.at[slot], core_peer))

    def mid_wait(slot):
        remote(mid_recv.at[slot], mid_recv.at[slot], mid_send_sem.at[0], mid_recv_sem.at[slot], mid_peer).wait_recv()

    def pass_on(k):
        slot = outer_at(k)
        mid_wait(slot)

        def step(j, carry):
            cols = columns(j)
            outer_send[slot, :, cols] = (
                own_sum[slot, :, cols] + mid_recv[slot, :, cols].astype(jnp.float32)
            ).astype(jnp.bfloat16)
            return carry

        lax.fori_loop(0, chunks, step, 0)
        go(remote(outer_send.at[slot], outer_recv.at[out], outer_send_sem.at[k], outer_recv_sem.at[out], outer_peer(k)))

    for k, back in zip(order, list(reversed(order))):
        forward_outer(k)
        pass_on(back)
    for k in [0] + order:
        forward_mid(k)
    for k in range(outer):
        for m in range(MID):
            arrival(at(outer_at(k), m, 1 - core)).wait_recv()

    half = n // 2
    group = max(1, min(half, 256 // rows))

    def part_step(base, target):
        def step(g, carry):
            some = weights[pl.ds(base + g * group, group)].reshape(group * rows, ff)
            target[g] = lax.dot_general(
                hid[...], some, (((1,), (1,)), ((), ())), preferred_element_type=jnp.float32
            )
            return carry

        lax.fori_loop(0, half // group, step, 0)

    part_step((1 - rep) * half, part_send)
    part_copy = go(remote(part_send, part_recv, part_send_sem, part_recv_sem, rep_peer))

    def input_step(j, carry):
        cols = columns(j)
        grad = jnp.dot(
            cot_ref[...], weights[:, :, cols].reshape(n * rows, width),
            preferred_element_type=jnp.float32,
        )
        gate = gate_ref[:, cols].astype(jnp.float32)
        up_val = up_ref[:, cols].astype(jnp.float32)
        sig = jax.nn.sigmoid(gate)
        gate_grad_ref[:, cols] = (grad * up_val * sig * (1.0 + gate * (1.0 - sig))).astype(jnp.bfloat16)
        up_grad_ref[:, cols] = (grad * gate * sig).astype(jnp.bfloat16)
        return carry

    lax.fori_loop(0, chunks, input_step, 0)

    part_copy.wait_recv()
    base = rep * half
    for g in range(half // group):
        some = weights[pl.ds(base + g * group, group)].reshape(group * rows, ff)
        own = lax.dot_general(
            hid[...], some, (((1,), (1,)), ((), ())), preferred_element_type=jnp.float32
        )
        out_ref[:, g * group * rows : (g + 1) * group * rows] = (own + part_recv[g]).astype(jnp.bfloat16)

    mid_wait(out)
    sources = [lax.rem(out + outer - k, outer) for k in range(1, outer)]
    for source in sources:
        remote(outer_recv.at[source], outer_recv.at[source], outer_send_sem.at[0], outer_recv_sem.at[source], mid_peer).wait_recv()

    def update_step(j, carry):
        cols = columns(j)
        grad = own_sum[out, :, cols] + mid_recv[out, :, cols].astype(jnp.float32)
        for source in sources:
            grad += outer_recv[source, :, cols].astype(jnp.float32)
        master_new, first, second = adam(
            grad / jnp.float32(total), master_ref[:, cols], one_ref[:, cols], two_ref[:, cols]
        )
        master_new_ref[:, cols] = master_new
        first_ref[:, cols] = first
        second_ref[:, cols] = second
        return carry

    lax.fori_loop(0, chunks, update_step, 0)
    for copy in started:
        copy.wait_send()


def in_one_kernel(size, gate_pre, up_pre, out_grad, master, moment_one, moment_two):
    micro, count, ff = gate_pre.shape
    tokens, depth, rows = micro * count, out_grad.shape[2], master.shape[0]
    outer = size // (MID * CORES)
    half = size // 2
    group = max(1, min(half, 256 // rows))
    cot = out_grad.reshape(tokens, depth)
    cot_rows = jnp.transpose(cot.reshape(tokens, outer, MID, CORES, rows), (3, 2, 1, 4, 0))
    vmem = pl.BlockSpec(memory_space=pltpu.VMEM)
    bf, f32 = jnp.bfloat16, jnp.float32
    dma = pltpu.SemaphoreType.DMA
    results = pl.pallas_call(
        functools.partial(fused, outer, tokens * size),
        out_shape=(
            jax.ShapeDtypeStruct((tokens, depth // 2), bf),
            jax.ShapeDtypeStruct((tokens, ff), bf),
            jax.ShapeDtypeStruct((tokens, ff), bf),
            jax.ShapeDtypeStruct((rows, ff), f32),
            jax.ShapeDtypeStruct((rows, ff), f32),
            jax.ShapeDtypeStruct((rows, ff), f32),
        ),
        in_specs=[vmem] * 8,
        out_specs=(vmem,) * 6,
        scratch_shapes=[
            pltpu.VMEM((size, rows, ff), bf),
            pltpu.VMEM((tokens, ff), bf),
            pltpu.VMEM((tokens, ff), bf),
            pltpu.VMEM((MID, outer, rows, tokens), bf),
            pltpu.VMEM((outer, rows, ff), f32),
            pltpu.VMEM((outer, rows, ff), bf),
            pltpu.VMEM((outer, rows, ff), bf),
            pltpu.VMEM((outer, rows, ff), bf),
            pltpu.VMEM((outer, rows, ff), bf),
            pltpu.VMEM((half // group, tokens, group * rows), f32),
            pltpu.VMEM((half // group, tokens, group * rows), f32),
            dma((size,)), dma((outer,)), dma((outer,)), dma((2 * outer,)),
            dma((2,)), dma((2,)),
            dma((outer,)), dma((outer,)), dma((outer,)), dma((outer,)), dma, dma,
        ],
        compiler_params=pltpu.CompilerParams(
            collective_id=0, has_side_effects=True, vmem_limit_bytes=60 * 1024 * 1024
        ),
    )(
        gate_pre.reshape(tokens, ff), up_pre.reshape(tokens, ff), cot, cot_rows,
        master.astype(bf), master, moment_one, moment_two,
    )
    split = [value.reshape(micro, count, value.shape[1]) for value in results[:3]]
    return (*split, *results[3:])


def with_collectives(gate_pre, up_pre, out_grad, master, moment_one, moment_two):
    weights = lax.all_gather(master.astype(jnp.bfloat16), "dp", axis=0, tiled=True)
    micro = gate_pre.shape[0]
    total = micro * gate_pre.shape[1] * lax.axis_size("dp")
    outs_list = []
    gate_list = []
    up_list = []
    grad_sum = None
    for index in range(micro):
        gate = gate_pre[index].astype(jnp.float32)
        up_val = up_pre[index].astype(jnp.float32)
        sig = jax.nn.sigmoid(gate)
        hidden = (gate * sig * up_val).astype(jnp.bfloat16)
        partial_out = lax.dot_general(
            hidden, weights, (((1,), (1,)), ((), ())), preferred_element_type=jnp.float32
        )
        outs_list.append(
            lax.psum_scatter(partial_out, "rep", scatter_dimension=1, tiled=True).astype(
                jnp.bfloat16
            )
        )
        hid_grad = jnp.dot(out_grad[index], weights, preferred_element_type=jnp.float32)
        gate_list.append(
            (hid_grad * up_val * sig * (1.0 + gate * (1.0 - sig))).astype(jnp.bfloat16)
        )
        up_list.append((hid_grad * gate * sig).astype(jnp.bfloat16))
        term = lax.dot_general(
            out_grad[index], hidden, (((0,), (0,)), ((), ())), preferred_element_type=jnp.float32
        )
        shard = lax.psum_scatter(term, "dp", scatter_dimension=0, tiled=True)
        grad_sum = shard if grad_sum is None else grad_sum + shard
    updated = adam(grad_sum / jnp.float32(total), master, moment_one, moment_two)
    return jnp.stack(outs_list), jnp.stack(gate_list), jnp.stack(up_list), *updated


def solution(mesh):
    size = mesh.shape["dp"]

    def on_device(gate_pre, up_pre, out_grad, master, moment_one, moment_two):
        tall = master.shape[0] % 16 == 0 and size % (MID * CORES) == 0
        step = functools.partial(in_one_kernel, size) if tall else with_collectives
        return step(gate_pre, up_pre, out_grad, master, moment_one, moment_two)

    split = P(None, "dp", "rep")
    owned = P("dp", "rep")
    return jax.shard_map(
        on_device,
        mesh=mesh,
        in_specs=(split, split, P(None, "dp", None), owned, owned, owned),
        out_specs=(split, split, split, owned, owned, owned),
        check_vma=False,
    )
```

time: 265 us -> 106 us (0.40)
  waiting for transfers between devices: 203 us -> 0 us
  Pallas kernels: 0 us -> 92.1 us
  matrix products: 25.9 us -> 0 us
  between operations: 13.9 us -> 0.66 us
  other arithmetic: 8.28 us -> 1.94 us
    reduce_scatter x3 -> x0, waiting for transfers between devices: 145 us -> none  [the longest x1 130 us: on_device(): lax.psum_scatter(single_term(jnp.int32(0), lax.axis_size('dp') * own_rows...]
    pallas_call x0 -> x1, Pallas kernels: none -> 92.1 us  [in_one_kernel(): pl.pallas_call(functools.partial(fused, outer, tokens * size), out_shape=...]
    all_gather x1 -> x0, waiting for transfers between devices: 58.1 us -> none  [on_device(): weights = lax.all_gather(shard_bf, 'dp', axis=0, tiled=True)]
    dot_general x6 -> x0, matrix products: 25.9 us -> none  [the longest x2 10.9 us: on_device(): lax.dot_general(hidden, weights, (((1,), (1,)), ((), ())), preferred_elem...]
    another operation x4 -> x0, other arithmetic: 4.49 us -> none  [the longest x3 2.66 us: on_device(): jnp.stack(outs_list)]
    unnamed x13 -> x16, local copies, waits for them, and re-layouts: 13 us -> 8.53 us
    sub x1 -> x0, other arithmetic: 3.79 us -> none  [on_device(): master_new = master - 0.003 * (update + 0.1 * master)]
    another operation x0 -> x2, local copies, waits for them, and re-layouts: none -> 2.97 us  [in_one_kernel(): cot.reshape(tokens, outer, MID, CORES, rows)]
  transfers between devices with their start and end apart: 4 -> 0, of which waited for: 3 -> 0; matrix products, arithmetic and copies ran while one was open for 5% -> 0% of each run, Pallas kernels for 0% -> 0%
where the time goes in v1:
time: 106 us
  Pallas kernels  92.1 us (87%)
  local copies, waits for them, and re-layouts  11.5 us (11%)
  other arithmetic  1.94 us (2%)
    pallas_call x1, Pallas kernels, in_one_kernel(): pl.pallas_call(functools.partial(fused, outer, tokens * size), out_shape=...  92.1 us
    unnamed x16, local copies, waits for them, and re-layouts  8.53 us
    another operation x2, local copies, waits for them, and re-layouts, in_one_kernel(): cot.reshape(tokens, outer, MID, CORES, rows)  2.97 us

profile of v1, /device:TPU:0, one launch (start us, length us, event | category | flops | bytes accessed | tf_op | source)
XLA Modules:
  0.0 106.2 jit_solution(2035186944837289164)
XLA Ops:
  0.6 0.0 copy-start
  0.6 1.9 %convert_element_type.3.shard_ref = bf16[64,2816]{1,0:T(8,128)(2,1)} convert(f32[64,2816]{1,0:T(8,128)} %master_ref.1) | non-fusion elementwise | flops 180224 | bytes 1081344 | tf_op jit(solution)/shard_map/convert_element_type | solution.py:273
  2.6 0.0 copy-done
  2.6 0.7 reshape.36
  3.2 2.3 %copy.13 = bf16[256,4,2,2,64]{0,4,1,2,3:T(8,128)(2,1)} copy(bf16[256,4,2,2,64]{4,3,2,1,0:T(2,128)(2,1)S(1)} %reshape.36) | data formatting | bytes 1048576 | tf_op jit(solution)/shard_map/reshape;reshape | solution.py:236
  5.6 92.1 %shard_map.109 = (bf16[256,512]{1,0:T(8,128)(2,1)}, bf16[256,2816]{1,0:T(8,128)(2,1)}, bf16[256,2816]{1,0:T(8,128)(2,1)}, f32[64,2816]{1,0:T(8,128)}, f32[64,2816]{1,0:T(8,128)}, /*index=5*/f32[64,2816]{1,0:T(8,128)}) custom-call(bf16[256,2816]{1,0:T(8,128)(2,1)} %bitcast.11, bf16[256,2816]{1,0:T(8,128)(2,1)} %bitcast.12, bf16[256,1024]{1,0:T(8,128)(2,1)} %bitcast.7, ...), custom_call_target="tpu_custom_call" | custom-call | tf_op jit(solution)/shard_map/pallas_call | solution.py:240
  97.7 1.7 %copy.22 = bf16[2,128,512]{2,1,0:T(8,128)(2,1)} copy(bf16[2,128,512]{2,1,0:T(8,128)(2,1)} %bitcast.13) | data formatting | bytes 524288
  99.4 0.0 copy-start.1
  99.4 2.7 %copy.23 = bf16[2,128,2816]{2,1,0:T(8,128)(2,1)} copy(bf16[2,128,2816]{2,1,0:T(8,128)(2,1)} %bitcast.10) | data formatting | bytes 2883584
  102.0 0.0 copy-done.1
  102.0 0.0 copy-start.4
  102.0 0.0 copy-start.3
  102.0 1.1 %copy.24 = bf16[2,128,2816]{2,1,0:T(8,128)(2,1)} copy(bf16[2,128,2816]{2,1,0:T(8,128)(2,1)S(1)} %bitcast.9) | data formatting | bytes 2883584
  103.1 0.5 copy-done.4
  103.6 0.0 copy-start.2
  103.6 0.9 copy.25
  104.5 0.0 copy-done.3
  104.5 0.9 copy.26
  105.4 0.0 copy-done.2
  105.4 0.9 copy.27
Async XLA Ops:
  0.6 2.0 %copy-start = (bf16[2,128,1024]{2,1,0:T(8,128)(2,1)S(1)}, bf16[2,128,1024]{2,1,0:T(8,128)(2,1)}, u32[]{:S(2)}) copy-start(bf16[2,128,1024]{2,1,0:T(8,128)(2,1)} %param.8) | copy-start | bytes 1572868
  99.4 2.7 %copy-start.1 = (bf16[256,2816]{1,0:T(8,128)(2,1)S(1)}, bf16[256,2816]{1,0:T(8,128)(2,1)}, u32[]{:S(2)}) copy-start(bf16[256,2816]{1,0:T(8,128)(2,1)} %get-tuple-element.14) | copy-start | bytes 4325380
  102.0 1.6 %copy-start.4 = (f32[64,2816]{1,0:T(8,128)S(1)}, f32[64,2816]{1,0:T(8,128)}, u32[]{:S(2)}) copy-start(f32[64,2816]{1,0:T(8,128)} %get-tuple-element.27) | copy-start | bytes 2162692
  102.0 2.5 %copy-start.3 = (f32[64,2816]{1,0:T(8,128)S(1)}, f32[64,2816]{1,0:T(8,128)}, u32[]{:S(2)}) copy-start(f32[64,2816]{1,0:T(8,128)} %get-tuple-element.28) | copy-start | bytes 2162692
  103.6 1.7 %copy-start.2 = (f32[64,2816]{1,0:T(8,128)S(1)}, f32[64,2816]{1,0:T(8,128)}, u32[]{:S(2)}) copy-start(f32[64,2816]{1,0:T(8,128)} %get-tuple-element.29) | copy-start | bytes 2162692

commit v2 on v1

--- a/solution.py
+++ b/solution.py
@@ -24,10 +24,10 @@
 
 def fused(
     outer, total,
-    gate_ref, up_ref, cot_ref, cot_rows_ref, shard_ref, master_ref, one_ref, two_ref,
+    gate_hbm, up_hbm, cot_ref, master_ref, one_hbm, two_hbm,
     out_ref, gate_grad_ref, up_grad_ref, master_new_ref, first_ref, second_ref,
     weights, hid, hid_peer, cot_peer, own_sum, mid_send, mid_recv, outer_send, outer_recv,
-    part_send, part_recv,
+    part_send, part_recv, cot_rows_ref, gate_ref, up_ref, one_ref, two_ref, local_sem,
     w_recv, w_mid_send, w_outer_send, w_core_send,
     core_send_sem, core_recv_sem,
     mid_send_sem, mid_recv_sem, outer_send_sem, outer_recv_sem, part_send_sem, part_recv_sem,
@@ -38,8 +38,16 @@
     mid = lax.rem(me // CORES, MID)
     out = me // (CORES * MID)
     n = outer * MID * CORES
-    rows, ff = shard_ref.shape
+    rows, ff = master_ref.shape
     tokens = gate_ref.shape[0]
+    loads = [
+        pltpu.make_async_copy(src, dst, local_sem.at[index])
+        for index, (src, dst) in enumerate(
+            ((gate_hbm, gate_ref), (up_hbm, up_ref), (one_hbm, one_ref), (two_hbm, two_ref))
+        )
+    ]
+    for load in loads:
+        load.start()
     width = 256 if ff % 256 == 0 else 128
     chunks = ff // width
 
@@ -62,6 +70,7 @@
             device_id=device, device_id_type=MESH,
         )
 
+    weights[me] = master_ref[...].astype(jnp.bfloat16)
     barrier = pltpu.get_barrier_semaphore()
     peers = [core_peer, mid_peer, rep_peer] + [outer_peer(k) for k in range(1, outer)]
     for peer in peers:
@@ -77,11 +86,16 @@
         return copy
 
     for k in order:
-        go(remote(shard_ref, weights.at[me], w_outer_send.at[k], w_recv.at[me], outer_peer(k)))
-    go(remote(shard_ref, weights.at[me], w_mid_send.at[0], w_recv.at[me], mid_peer))
-    go(remote(shard_ref, weights.at[me], w_core_send.at[0], w_recv.at[me], core_peer))
-    cot_copy = go(remote(cot_rows_ref.at[1 - core], cot_peer, core_send_sem.at[0], core_recv_sem.at[0], core_peer))
-    weights[me] = shard_ref[...]
+        go(remote(weights.at[me], weights.at[me], w_outer_send.at[k], w_recv.at[me], outer_peer(k)))
+    go(remote(weights.at[me], weights.at[me], w_mid_send.at[0], w_recv.at[me], mid_peer))
+    go(remote(weights.at[me], weights.at[me], w_core_send.at[0], w_recv.at[me], core_peer))
+    turned = jnp.transpose(cot_ref[...].astype(jnp.float32)).astype(jnp.bfloat16).reshape(n, rows, tokens)
+    for o in range(outer):
+        for m in range(MID):
+            for c in range(CORES):
+                cot_rows_ref[c, m, o] = turned[at(o, m, c)]
+    loads[0].wait()
+    loads[1].wait()
 
     def columns(j):
         return pl.ds(pl.multiple_of(j * width, width), width)
@@ -94,6 +108,7 @@
         return carry
 
     lax.fori_loop(0, chunks, hidden_step, 0)
+    cot_copy = go(remote(cot_rows_ref.at[1 - core], cot_peer, core_send_sem.at[0], core_recv_sem.at[0], core_peer))
     hid_copy = go(remote(hid, hid_peer, core_send_sem.at[1], core_recv_sem.at[1], core_peer))
     cot_copy.wait_recv()
     hid_copy.wait_recv()
@@ -111,17 +126,10 @@
         return carry
 
     lax.fori_loop(0, chunks, send_step, 0)
-    shift = list(reversed(order)) + [0]
-    for k in shift:
+
+    def reduce_mid(k):
         slot = outer_at(k)
         go(remote(mid_send.at[slot], mid_recv.at[slot], mid_send_sem.at[k], mid_recv_sem.at[slot], mid_peer))
-
-    def own_step(j, carry):
-        cols = columns(j)
-        own_sum[:, :, cols] = grad_of(mid, cols)
-        return carry
-
-    lax.fori_loop(0, chunks, own_step, 0)
 
     def arrival(slot):
         return remote(weights.at[slot], weights.at[slot], w_core_send.at[0], w_recv.at[slot], core_peer)
@@ -154,11 +162,28 @@
         lax.fori_loop(0, chunks, step, 0)
         go(remote(outer_send.at[slot], outer_recv.at[out], outer_send_sem.at[k], outer_recv_sem.at[out], outer_peer(k)))
 
-    for k, back in zip(order, list(reversed(order))):
-        forward_outer(k)
-        pass_on(back)
-    for k in [0] + order:
+    back = list(reversed(order))
+    forward_outer(order[0])
+    reduce_mid(back[0])
+    def own_step(j, carry):
+        cols = columns(j)
+        own_sum[:, :, cols] = grad_of(mid, cols)
+        return carry
+
+    lax.fori_loop(0, chunks, own_step, 0)
+
+    forward_mid(0)
+    for index in range(1, outer - 1):
+        forward_outer(order[index])
+        reduce_mid(back[index])
+        if index < outer - 2:
+            pass_on(back[index - 1])
+    reduce_mid(0)
+    for k in order[:-1]:
         forward_mid(k)
+    if outer > 2:
+        pass_on(back[-2])
+    forward_mid(order[-1])
     for k in range(outer):
         for m in range(MID):
             arrival(at(outer_at(k), m, 1 - core)).wait_recv()
@@ -192,7 +217,9 @@
         up_grad_ref[:, cols] = (grad * gate * sig).astype(jnp.bfloat16)
         return carry
 
-    lax.fori_loop(0, chunks, input_step, 0)
+    lax.fori_loop(0, chunks // 2, input_step, 0)
+    pass_on(back[-1])
+    lax.fori_loop(chunks // 2, chunks, input_step, 0)
 
     part_copy.wait_recv()
     base = rep * half
@@ -207,6 +234,9 @@
     sources = [lax.rem(out + outer - k, outer) for k in range(1, outer)]
     for source in sources:
         remote(outer_recv.at[source], outer_recv.at[source], outer_send_sem.at[0], outer_recv_sem.at[source], mid_peer).wait_recv()
+
+    loads[2].wait()
+    loads[3].wait()
 
     def update_step(j, carry):
         cols = columns(j)
@@ -233,8 +263,8 @@
     half = size // 2
     group = max(1, min(half, 256 // rows))
     cot = out_grad.reshape(tokens, depth)
-    cot_rows = jnp.transpose(cot.reshape(tokens, outer, MID, CORES, rows), (3, 2, 1, 4, 0))
     vmem = pl.BlockSpec(memory_space=pltpu.VMEM)
+    hbm = pl.BlockSpec(memory_space=pl.ANY)
     bf, f32 = jnp.bfloat16, jnp.float32
     dma = pltpu.SemaphoreType.DMA
     results = pl.pallas_call(
@@ -247,7 +277,7 @@
             jax.ShapeDtypeStruct((rows, ff), f32),
             jax.ShapeDtypeStruct((rows, ff), f32),
         ),
-        in_specs=[vmem] * 8,
+        in_specs=[hbm, hbm, vmem, vmem, hbm, hbm],
         out_specs=(vmem,) * 6,
         scratch_shapes=[
             pltpu.VMEM((size, rows, ff), bf),
@@ -261,6 +291,12 @@
             pltpu.VMEM((outer, rows, ff), bf),
             pltpu.VMEM((half // group, tokens, group * rows), f32),
             pltpu.VMEM((half // group, tokens, group * rows), f32),
+            pltpu.VMEM((CORES, MID, outer, rows, tokens), bf),
+            pltpu.VMEM((tokens, ff), bf),
+            pltpu.VMEM((tokens, ff), bf),
+            pltpu.VMEM((rows, ff), f32),
+            pltpu.VMEM((rows, ff), f32),
+            dma((4,)),
             dma((size,)), dma((outer,)), dma((outer,)), dma((2 * outer,)),
             dma((2,)), dma((2,)),
             dma((outer,)), dma((outer,)), dma((outer,)), dma((outer,)), dma, dma,
@@ -269,8 +305,7 @@
             collective_id=0, has_side_effects=True, vmem_limit_bytes=60 * 1024 * 1024
         ),
     )(
-        gate_pre.reshape(tokens, ff), up_pre.reshape(tokens, ff), cot, cot_rows,
-        master.astype(bf), master, moment_one, moment_two,
+        gate_pre.reshape(tokens, ff), up_pre.reshape(tokens, ff), cot, master, moment_one, moment_two,
     )
     split = [value.reshape(micro, count, value.shape[1]) for value in results[:3]]
     return (*split, *results[3:])
@@ -315,7 +350,7 @@
     size = mesh.shape["dp"]
 
     def on_device(gate_pre, up_pre, out_grad, master, moment_one, moment_two):
-        tall = master.shape[0] % 16 == 0 and size % (MID * CORES) == 0
+        tall = master.shape[0] % 16 == 0 and size % (MID * CORES) == 0 and size > MID * CORES
         step = functools.partial(in_one_kernel, size) if tall else with_collectives
         return step(gate_pre, up_pre, out_grad, master, moment_one, moment_two)
 

time: 106 us -> 90.8 us (0.86)
  the two profiles are of different devices: /device:TPU:0 before, /device:TPU:17 now
where the time goes in v2:
time: 90.8 us; the launch traced here: 90.6 us
  Pallas kernels  81.4 us (90%)
  local copies, waits for them, and re-layouts  8.52 us (9%)
    pallas_call x1, Pallas kernels, in_one_kernel(): pl.pallas_call(functools.partial(fused, outer, tokens * size), out_shape=...  81.4 us
    unnamed x14, local copies, waits for them, and re-layouts  8.52 us

profile of v2, /device:TPU:17, one launch (start us, length us, event | category | flops | bytes accessed | tf_op | source)
XLA Modules:
  0.0 90.6 jit_solution(16518159447546209972)
XLA Ops:
  0.6 81.4 %shard_map.109 = (bf16[256,512]{1,0:T(8,128)(2,1)}, bf16[256,2816]{1,0:T(8,128)(2,1)}, bf16[256,2816]{1,0:T(8,128)(2,1)}, f32[64,2816]{1,0:T(8,128)}, f32[64,2816]{1,0:T(8,128)}, /*index=5*/f32[64,2816]{1,0:T(8,128)}) custom-call(bf16[256,2816]{1,0:T(8,128)(2,1)} %bitcast.8, bf16[256,2816]{1,0:T(8,128)(2,1)} %bitcast.9, bf16[256,1024]{1,0:T(8,128)(2,1)} %bitcast.10, ...), custom_call_target="tpu_custom_call" | custom-call | tf_op jit(solution)/shard_map/pallas_call | solution.py:270
  82.0 1.7 %copy.18 = bf16[2,128,512]{2,1,0:T(8,128)(2,1)} copy(bf16[2,128,512]{2,1,0:T(8,128)(2,1)} %bitcast.11) | data formatting | bytes 524288
  83.7 0.0 copy-start
  83.7 2.7 %copy.19 = bf16[2,128,2816]{2,1,0:T(8,128)(2,1)} copy(bf16[2,128,2816]{2,1,0:T(8,128)(2,1)} %bitcast.7) | data formatting | bytes 2883584
  86.4 0.0 copy-done
  86.4 0.0 copy-start.3
  86.4 0.0 copy-start.2
  86.4 1.1 %copy.20 = bf16[2,128,2816]{2,1,0:T(8,128)(2,1)} copy(bf16[2,128,2816]{2,1,0:T(8,128)(2,1)S(1)} %bitcast.6) | data formatting | bytes 2883584
  87.5 0.5 copy-done.3
  88.0 0.0 copy-start.1
  88.0 0.9 copy.21
  88.8 0.0 copy-done.2
  88.8 0.9 copy.22
  89.7 0.0 copy-done.1
  89.7 0.9 copy.23
Async XLA Ops:
  83.7 2.7 %copy-start = (bf16[256,2816]{1,0:T(8,128)(2,1)S(1)}, bf16[256,2816]{1,0:T(8,128)(2,1)}, u32[]{:S(2)}) copy-start(bf16[256,2816]{1,0:T(8,128)(2,1)} %get-tuple-element.14) | copy-start | bytes 4325380
  86.4 1.6 %copy-start.3 = (f32[64,2816]{1,0:T(8,128)S(1)}, f32[64,2816]{1,0:T(8,128)}, u32[]{:S(2)}) copy-start(f32[64,2816]{1,0:T(8,128)} %get-tuple-element.27) | copy-start | bytes 2162692
  86.4 2.5 %copy-start.2 = (f32[64,2816]{1,0:T(8,128)S(1)}, f32[64,2816]{1,0:T(8,128)}, u32[]{:S(2)}) copy-start(f32[64,2816]{1,0:T(8,128)} %get-tuple-element.28) | copy-start | bytes 2162692
  88.0 1.7 %copy-start.1 = (f32[64,2816]{1,0:T(8,128)S(1)}, f32[64,2816]{1,0:T(8,128)}, u32[]{:S(2)}) copy-start(f32[64,2816]{1,0:T(8,128)} %get-tuple-element.29) | copy-start | bytes 2162692
